TPU v7x, 32 devices: a whole 2x2x4 slice. The times are simulated.
32 devices in a mesh: space: 2 (over x), energy: 16 (over z, y, core).
Axes of the slice: x: 2, y: 2, z: 4, core: 2. Of those that a mesh axis runs over, the one named last changes fastest.
Arguments:
- lesser_in: bfloat16 [16, 2, 2, 256, 256], P('energy', 'space'), may hold values from -6 to 6
- retarded: bfloat16 [16, 2, 2, 256, 256], P('energy', 'space'), may hold values from -0.25 to 0.25
- coupling: bfloat16 [2, 2, 256, 256], P('space'), may hold values from -0.25 to 0.25
- interaction: bfloat16 [2, 32, 65536], P('space', None, 'energy'), may hold values from -1.5 to 1.5
Outputs:
- self_energy: bfloat16 [16, 2, 2, 256, 256], P('energy', 'space')
All inputs are finite; a program needn't handle non-finite values.
Results may differ from a plain program's by a relative error of at most 0.029.
Values may be sent and summed in bfloat16 or wider, within the bound.
A program may use at most 128 MiB of HBM per device.

v0:
```python
import functools
import math

import jax
import jax.numpy as jnp
import numpy as np
from jax import lax
from jax.experimental import pallas as pl
from jax.experimental.pallas import tpu as pltpu
from jax.sharding import PartitionSpec as P

MESH = pl.DeviceIdType.MESH
ANY = pl.BlockSpec(memory_space=pl.ANY)


def phase_parts(row_count, column_count, length):
    residue = np.arange(row_count)[:, None] * np.arange(column_count)[None, :] % length
    phase = residue * (2.0 * math.pi / length)
    return np.cos(phase), np.sin(phase)


def forward_matrix(energy_count, length, rows):
    cosine, sine = phase_parts(length, energy_count, length)
    small = np.array([[cosine, sine], [-sine, cosine]])
    full = np.einsum("pqfe,rs->rpfeqs", small, np.eye(rows))
    return full.reshape(rows * 2 * length, energy_count * 2 * rows).astype(jnp.bfloat16)


def inverse_matrix(energy_count, length, rows):
    cosine, sine = phase_parts(energy_count, length, length)
    small = np.array([[cosine, -sine], [sine, cosine]])
    full = np.einsum("pqef,rs->eprsqf", small, np.eye(rows))
    return full.reshape(energy_count * 2 * rows, rows * 2 * length).astype(jnp.bfloat16)


def dot(left, right):
    return jnp.dot(left, right, preferred_element_type=jnp.float32)


def dot_t(left, right):
    return lax.dot_general(
        left, right, (((1,), (1,)), ((), ())), preferred_element_type=jnp.float32
    )


def kernel(
    sections, groups, rows, length, pieces, parts,
    lesser_hbm, retarded_hbm, coupling_hbm, interaction_hbm, forward_hbm, inverse_hbm,
    out_hbm,
    lesser, retarded, coupling, interaction, forward, inverse,
    total, maps, green, before, homing, homed, weighted, leaving,
    load_sem, hop_send, hop_recv, go_send, go_recv, back_send, back_recv, own_sem,
):
    section = lax.axis_index("space")
    me = lax.axis_index("energy")
    order = green.shape[-1]
    width = order // pieces

    barrier = pltpu.get_barrier_semaphore()
    for step in range(1, groups):
        peer = lax.rem(me + step, groups)
        pl.semaphore_signal(barrier, inc=1, device_id={"energy": peer}, device_id_type=MESH)

    @pl.when(section > 0)
    def _():
        pl.semaphore_signal(barrier, inc=1, device_id={"space": section - 1}, device_id_type=MESH)

    @pl.when(section < sections - 1)
    def _():
        pl.semaphore_signal(barrier, inc=1, device_id={"space": section + 1}, device_id_type=MESH)

    loads = []
    for at, (source, target) in enumerate((
        (retarded_hbm.at[0, 0], retarded),
        (lesser_hbm.at[0, 0], lesser),
        (coupling_hbm.at[0], coupling),
        (interaction_hbm.at[0], interaction),
        (forward_hbm, forward),
        (inverse_hbm, inverse),
    )):
        load = pltpu.make_async_copy(source, target, load_sem.at[at])
        load.start()
        loads.append(load)

    loads[0].wait()
    loads[1].wait()
    r_re, r_im = retarded[0], retarded[1]
    l_re, l_im = lesser[0], lesser[1]
    half_re = (dot(r_re, l_re) - dot(r_im, l_im)).astype(jnp.bfloat16)
    half_im = (dot(r_re, l_im) + dot(r_im, l_re)).astype(jnp.bfloat16)
    total[0] = dot_t(half_re, r_re) + dot_t(half_im, r_im)
    total[1] = dot_t(half_im, r_re) - dot_t(half_re, r_im)

    pl.semaphore_wait(
        barrier,
        groups - 1 + jnp.where(section > 0, 1, 0) + jnp.where(section < sections - 1, 1, 0),
    )
    loads[2].wait()

    def hop(piece, target):
        columns = pl.ds(piece * width, width)
        return pltpu.make_async_remote_copy(
            src_ref=green.at[:, :, columns],
            dst_ref=before.at[:, :, columns],
            send_sem=hop_send.at[piece],
            recv_sem=hop_recv.at[piece],
            device_id={"space": target},
            device_id_type=MESH,
        )

    @pl.when(section > 0)
    def _():
        c_re, c_im = coupling[0], coupling[1]
        maps[0] = (dot(r_re, c_re) - dot(r_im, c_im)).astype(jnp.bfloat16)
        maps[1] = (dot(r_re, c_im) + dot(r_im, c_re)).astype(jnp.bfloat16)
        for piece in range(pieces):
            hop(piece, section - 1).wait_recv()
            part = slice(piece * width, (piece + 1) * width)
            b_re, b_im = before[0, :, part], before[1, :, part]
            m_re, m_im = maps[0], maps[1]
            k_re = (dot(m_re, b_re) - dot(m_im, b_im)).astype(jnp.bfloat16)
            k_im = (dot(m_re, b_im) + dot(m_im, b_re)).astype(jnp.bfloat16)
            n_re, n_im = maps[0, :, part], maps[1, :, part]
            total[0] += dot_t(k_re, n_re) + dot_t(k_im, n_im)
            total[1] += dot_t(k_im, n_re) - dot_t(k_re, n_im)

    @pl.when(section < sections - 1)
    def _():
        green[...] = total[...].astype(jnp.bfloat16)
        for piece in range(pieces):
            hop(piece, section + 1).start()

    share = rows // parts
    for part in range(parts):
        homing[part] = jnp.concatenate(
            [
                total[side].reshape(groups, parts, share, order)[:, part]
                for side in range(2)
            ],
            axis=1,
        ).astype(jnp.bfloat16)

    def go(part, peer, slot):
        return pltpu.make_async_remote_copy(
            src_ref=homing.at[part, peer],
            dst_ref=homed.at[part, slot],
            send_sem=go_send.at[part, peer],
            recv_sem=go_recv.at[part, slot],
            device_id={"energy": peer},
            device_id_type=MESH,
        )

    def back(part, peer, slot):
        return pltpu.make_async_remote_copy(
            src_ref=leaving.at[part, peer],
            dst_ref=out_hbm.at[slot, part],
            send_sem=back_send.at[part, peer],
            recv_sem=back_recv.at[part, slot],
            device_id={"energy": peer},
            device_id_type=MESH,
        )

    peers = [lax.rem(me + step, groups) for step in range(1, groups)]
    kept = []
    for part in range(parts):
        for peer in peers:
            go(part, peer, me).start()
        own = pltpu.make_async_copy(homing.at[part, me], homed.at[part, me], own_sem.at[0, part])
        own.start()
        kept.append(own)
    for load in loads[3:]:
        load.wait()

    stride = 2 * length
    chunk = max(1, order // stride)
    returns = []
    for part in range(parts):
        kept[part].wait()
        for peer in peers:
            go(part, peer, peer).wait_recv()
        entries = homed[part]
        if 2 * share % 16:
            entries = entries.astype(jnp.float32)
        entries = entries.reshape(groups * 2 * share, order).astype(jnp.bfloat16)
        for first in range(0, share, chunk):
            spectrum = dot(forward[first * stride:(first + chunk) * stride, :], entries)
            spectrum = spectrum * groups ** -0.5
            for at in range(chunk):
                row = first + at
                s_re = spectrum[at * stride:at * stride + length]
                s_im = spectrum[at * stride + length:(at + 1) * stride]
                entry = (part * share + row) * order
                weight = interaction[:, entry:entry + order].astype(jnp.float32)
                weighted[row * stride:row * stride + length, :] = (
                    (s_re * s_re - s_im * s_im) * weight
                ).astype(jnp.bfloat16)
                weighted[row * stride + length:(row + 1) * stride, :] = (
                    2.0 * s_re * s_im * weight
                ).astype(jnp.bfloat16)
        result = dot(inverse[...], weighted[...]) * length ** -0.5
        leaving[part] = result.reshape(groups, 2 * share, order).astype(jnp.bfloat16)
        for peer in peers:
            back(part, peer, me).start()
        own = pltpu.make_async_copy(leaving.at[part, me], out_hbm.at[me, part], own_sem.at[1, part])
        own.start()
        returns.append(own)

    for part in range(parts):
        for peer in peers:
            go(part, peer, me).wait_send()

    @pl.when(section < sections - 1)
    def _():
        for piece in range(pieces):
            hop(piece, section + 1).wait_send()

    for part in range(parts):
        returns[part].wait()
        for peer in peers:
            back(part, peer, me).wait_send()
        for peer in peers:
            back(part, peer, peer).wait_recv()


def local(lesser_in, retarded, coupling, interaction):
    order = coupling.shape[-1]
    groups = lax.axis_size("energy")
    sections = lax.axis_size("space")
    length = interaction.shape[1]
    rows = order // groups
    pieces = 2
    parts = 2 if rows % 16 == 0 else 1
    share = rows // parts
    assert lesser_in.shape[0] == 1 and coupling.shape[0] == 1
    forward = jnp.asarray(forward_matrix(groups, length, share))
    inverse = jnp.asarray(inverse_matrix(groups, length, share))
    low, wide = jnp.bfloat16, jnp.float32
    dma = pltpu.SemaphoreType.DMA
    returned = pl.pallas_call(
        functools.partial(kernel, sections, groups, rows, length, pieces, parts),
        out_shape=jax.ShapeDtypeStruct((groups, parts, 2 * share, order), low),
        in_specs=[ANY] * 6,
        out_specs=ANY,
        scratch_shapes=[
            pltpu.VMEM((2, order, order), low),
            pltpu.VMEM((2, order, order), low),
            pltpu.VMEM((2, order, order), low),
            pltpu.VMEM(interaction.shape[1:], low),
            pltpu.VMEM(forward.shape, low),
            pltpu.VMEM(inverse.shape, low),
            pltpu.VMEM((2, order, order), wide),
            pltpu.VMEM((2, order, order), low),
            pltpu.VMEM((2, order, order), low),
            pltpu.VMEM((2, order, order), low),
            pltpu.VMEM((parts, groups, 2 * share, order), low),
            pltpu.VMEM((parts, groups, 2 * share, order), low),
            pltpu.VMEM((share * 2 * length, order), low),
            pltpu.VMEM((parts, groups, 2 * share, order), low),
            dma((6,)),
            dma((pieces,)),
            dma((pieces,)),
            dma((parts, groups)),
            dma((parts, groups)),
            dma((parts, groups)),
            dma((parts, groups)),
            dma((2, parts)),
        ],
        compiler_params=pltpu.CompilerParams(
            collective_id=0, has_side_effects=True
        ),
    )(lesser_in, retarded, coupling, interaction, forward, inverse)
    returned = returned.reshape(groups, parts, 2, share, order).transpose(2, 0, 1, 3, 4)
    return returned.reshape(1, 1, 2, order, order)


def solution(mesh):
    in_specs = (
        P("energy", "space", None, None, None),
        P("energy", "space", None, None, None),
        P("space", None, None, None),
        P("space", None, "energy"),
    )
    out_specs = P("energy", "space", None, None, None)
    return jax.shard_map(local, mesh=mesh, in_specs=in_specs, out_specs=out_specs, check_vma=False)
```

profile of v0, /device:TPU:3, one launch (start us, length us, event | category | flops | bytes accessed | tf_op | source)
XLA Modules:
  0.0 28.2 jit_solution(5093067257417413944)
XLA Ops:
  0.0 26.5 %shard_map.64 = bf16[16,2,16,256]{3,2,1,0:T(8,128)(2,1)} custom-call(bf16[1,1,2,256,256]{4,3,2,1,0:T(8,128)(2,1)} %lesser_hbm.1, bf16[1,1,2,256,256]{4,3,2,1,0:T(8,128)(2,1)} %retarded_hbm.1, bf16[1,2,256,256]{3,2,1,0:T(8,128)(2,1)} %coupling_hbm.1, bf16[1,32,4096]{2,1,0:T(8,128)(2,1)} %interaction_hbm.1, bf16[512,256]{1,0:T(8,128)(2,1)} %constant.4.clone.forward_hbm, ...), custom_call_target="tpu_custom_call" | custom-call | tf_op jit(solution)/shard_map/pallas_call | solution.py:239
  26.5 1.7 %copy.7 = bf16[2,16,2,8,256]{4,3,2,1,0:T(8,128)(2,1)} copy(bf16[2,16,2,8,256]{4,3,0,2,1:T(8,128)(2,1)} %bitcast.4) | data formatting | bytes 524288 | tf_op jit(solution)/shard_map/transpose | solution.py:272
where the time goes:
time: 28.3 us; the launch traced here: 28.2 us
  Pallas kernels  26.5 us (94%)
  local copies, waits for them, and re-layouts  1.67 us (6%)
    pallas_call x1, Pallas kernels, local(): pl.pallas_call(functools.partial(kernel, sections, groups, rows, length,...  26.5 us
    transpose x1, local copies, waits for them, and re-layouts, local(): returned.reshape(groups, parts, 2, share, order).transpose(2, 0, 1, 3, 4)  1.67 us

commit v1 on v0

v1 whole, which is shorter than its diff:
```python
import functools
import math

import jax
import jax.numpy as jnp
import numpy as np
from jax import lax
from jax.experimental import pallas as pl
from jax.experimental.pallas import tpu as pltpu
from jax.sharding import PartitionSpec as P

MESH = pl.DeviceIdType.MESH
ANY = pl.BlockSpec(memory_space=pl.ANY)
LOW, WIDE = jnp.bfloat16, jnp.float32


def phase_parts(row_count, column_count, length):
    residue = np.arange(row_count)[:, None] * np.arange(column_count)[None, :] % length
    phase = residue * (2.0 * math.pi / length)
    return np.cos(phase), np.sin(phase)


def forward_matrix(energies, length, rows):
    cosine, sine = phase_parts(length, max(energies) + 1, length)
    cosine, sine = cosine[:, energies], sine[:, energies]
    small = np.array([[cosine, sine], [-sine, cosine]])
    full = np.einsum("pqfe,rs->rpfeqs", small, np.eye(rows))
    return full.reshape(rows * 2 * length, len(energies) * 2 * rows).astype(LOW)


def inverse_matrix(energy_count, length, rows):
    cosine, sine = phase_parts(energy_count, length, length)
    small = np.array([[cosine, -sine], [sine, cosine]])
    full = np.einsum("pqef,rs->eprsqf", small, np.eye(rows))
    return full.reshape(energy_count * 2 * rows, rows * 2 * length).astype(LOW)


def dot(left, right):
    return jnp.dot(left, right, preferred_element_type=WIDE)


def dot_t(left, right):
    return lax.dot_general(left, right, (((1,), (1,)), ((), ())), preferred_element_type=WIDE)


def product(a_re, a_im, b_re, b_im):
    return dot(a_re, b_re) + dot(-a_im, b_im), dot(a_re, b_im) + dot(a_im, b_re)


def product_adjoint(a_re, a_im, b_re, b_im):
    return dot_t(a_re, b_re) + dot_t(a_im, b_im), dot_t(a_im, b_re) + dot_t(-a_re, b_im)


def flipped(index, mask):
    bit = 1
    while bit <= mask:
        if mask & bit:
            index = index + bit - 2 * bit * (index // bit % 2)
        bit *= 2
    return index


def kernel(
    sections, groups, rows, length, pieces, parts,
    lesser_hbm, retarded_hbm, coupling_hbm, interaction_hbm, forward_hbm, inverse_hbm,
    landed,
    lesser, retarded, coupling, interaction, forward, inverse,
    total, maps, green, before, theirs, carried, homing, homed, grown, weighted, leaving,
    load_sem, hop_send, hop_recv, map_send, map_recv, go_send, go_recv, late_send, late_recv,
    back_send, back_recv, own_sem,
):
    section = lax.axis_index("space")
    me = lax.axis_index("energy")
    order = green.shape[-1]
    width = order // pieces
    last = sections - 1
    split = sections > 1 and groups % 2 == 0
    half = groups // 2 if split else 0
    odd = me % 2 == 1 if split else me < 0
    is_last = section == last
    feeds = (section < last - 1) | ((section == last - 1) & ~odd)
    fed = (section > 0) & ((section < last) | ~odd)
    lends = is_last & odd & (section > 0)
    grows = (section == last - 1) & odd

    if groups & (groups - 1) == 0:
        peers = [flipped(me, mask) for mask in range(groups - 1, 0, -1)]
    else:
        peers = [lax.rem(me + step, groups) for step in range(1, groups)]

    barrier = pltpu.get_barrier_semaphore()
    for peer in peers:
        pl.semaphore_signal(barrier, inc=1, device_id={"energy": peer}, device_id_type=MESH)

    @pl.when(fed)
    def _():
        pl.semaphore_signal(barrier, inc=1, device_id={"space": section - 1}, device_id_type=MESH)

    if split:
        @pl.when(grows)
        def _():
            pl.semaphore_signal(barrier, inc=1, device_id={"space": last}, device_id_type=MESH)

        @pl.when(is_last)
        def _():
            for at in range(half):
                pl.semaphore_signal(
                    barrier, inc=1,
                    device_id={"space": last - 1, "energy": 2 * at + 1}, device_id_type=MESH,
                )

    loads = []
    for at, (source, target) in enumerate((
        (retarded_hbm.at[0, 0], retarded),
        (lesser_hbm.at[0, 0], lesser),
        (coupling_hbm.at[0], coupling),
        (interaction_hbm.at[0], interaction),
        (forward_hbm, forward),
        (inverse_hbm, inverse),
    )):
        load = pltpu.make_async_copy(source, target, load_sem.at[at])
        loads.append(load)
        if target is coupling:
            pl.when(section > 0)(load.start)
        else:
            load.start()

    def arrived():
        pl.semaphore_wait(
            barrier,
            groups - 1 + jnp.where(feeds, 1, 0) + jnp.where(lends, 1, 0)
            + jnp.where(grows, groups, 0),
        )

    def hop(piece):
        columns = pl.ds(piece * width, width)
        return pltpu.make_async_remote_copy(
            src_ref=green.at[:, :, columns],
            dst_ref=before.at[:, :, columns],
            send_sem=hop_send.at[piece],
            recv_sem=hop_recv.at[piece],
            device_id={"space": section + 1},
            device_id_type=MESH,
        )

    def lend(piece):
        lines = pl.ds(piece * width, width)
        return pltpu.make_async_remote_copy(
            src_ref=maps.at[:, lines, :],
            dst_ref=theirs.at[:, lines, :],
            send_sem=map_send.at[piece],
            recv_sem=map_recv.at[piece],
            device_id={"space": section - 1},
            device_id_type=MESH,
        )

    def make_maps():
        loads[2].wait()
        m_re, m_im = product(retarded[0], retarded[1], coupling[0], coupling[1])
        maps[0], maps[1] = m_re.astype(LOW), m_im.astype(LOW)

    loads[0].wait()

    @pl.when(lends)
    def _():
        make_maps()
        arrived()
        for piece in range(pieces):
            lend(piece).start()

    loads[1].wait()
    r_re, r_im = retarded[0], retarded[1]
    half_re, half_im = product(r_re, r_im, lesser[0], lesser[1])
    half_re, half_im = half_re.astype(LOW), half_im.astype(LOW)
    total[0], total[1] = product_adjoint(half_re, half_im, r_re, r_im)

    @pl.when(~lends)
    def _():
        arrived()

    @pl.when(fed)
    def _():
        make_maps()
        for piece in range(pieces):
            hop(piece).wait_recv()
            part = slice(piece * width, (piece + 1) * width)
            k_re, k_im = product(maps[0], maps[1], before[0, :, part], before[1, :, part])
            g_re, g_im = product_adjoint(
                k_re.astype(LOW), k_im.astype(LOW), maps[0, :, part], maps[1, :, part]
            )
            total[0] += g_re
            total[1] += g_im

    @pl.when(feeds | grows)
    def _():
        green[...] = total[...].astype(LOW)

    @pl.when(feeds)
    def _():
        for piece in range(pieces):
            hop(piece).start()

    share = rows // parts

    def scattered(values, target):
        for part in range(parts):
            target[part] = jnp.concatenate(
                [values[side].reshape(groups, parts, share, order)[:, part] for side in range(2)],
                axis=1,
            ).astype(LOW).reshape(groups, 2 * share, order)

    def go(part, peer, slot):
        return pltpu.make_async_remote_copy(
            src_ref=homing.at[part, peer],
            dst_ref=homed.at[part, slot],
            send_sem=go_send.at[part, peer],
            recv_sem=go_recv.at[part, slot],
            device_id={"energy": peer},
            device_id_type=MESH,
        )

    def late(part, peer, slot):
        return pltpu.make_async_remote_copy(
            src_ref=grown.at[part, peer],
            dst_ref=homed.at[part, groups + slot],
            send_sem=late_send.at[part, peer],
            recv_sem=late_recv.at[part, slot],
            device_id={"space": last, "energy": peer},
            device_id_type=MESH,
        )

    def back(part, peer, slot):
        return pltpu.make_async_remote_copy(
            src_ref=leaving.at[part, peer],
            dst_ref=landed.at[slot, part],
            send_sem=back_send.at[part, peer],
            recv_sem=back_recv.at[part, slot],
            device_id={"energy": peer},
            device_id_type=MESH,
        )

    scattered((total[0], total[1]), homing)
    kept = []
    for part in range(parts):
        for peer in peers:
            go(part, peer, me).start()
        own = pltpu.make_async_copy(homing.at[part, me], homed.at[part, me], own_sem.at[0, part])
        own.start()
        kept.append(own)

    if split:
        @pl.when(grows)
        def _():
            for piece in range(pieces):
                lend(piece).wait_recv()
                part = slice(piece * width, (piece + 1) * width)
                k_re, k_im = product(theirs[0, part, :], theirs[1, part, :], green[0], green[1])
                carried[0, part, :], carried[1, part, :] = k_re.astype(LOW), k_im.astype(LOW)
            g_re, g_im = product_adjoint(carried[0], carried[1], theirs[0], theirs[1])
            scattered((g_re, g_im), grown)
            for part in range(parts):
                for peer in peers + [me]:
                    late(part, peer, me // 2).start()

        @pl.when(~is_last)
        def _():
            for part in range(parts):
                homed[part, groups:] = jnp.zeros((half, 2 * share, order), LOW)

    for load in loads[3:]:
        load.wait()

    stride = 2 * length
    chunk = max(1, order // stride)
    returns = []
    for part in range(parts):
        kept[part].wait()
        for peer in peers:
            go(part, peer, peer).wait_recv()
        if split:
            @pl.when(is_last)
            def _():
                for at in range(half):
                    late(part, me, at).wait_recv()
        entries = homed[part]
        if 2 * share % 16:
            entries = entries.astype(WIDE)
        entries = entries.reshape((groups + half) * 2 * share, order).astype(LOW)
        for first in range(0, share, chunk):
            spectrum = dot(forward[first * stride:(first + chunk) * stride, :], entries)
            spectrum = spectrum * groups ** -0.5
            for at in range(chunk):
                row = first + at
                s_re = spectrum[at * stride:at * stride + length]
                s_im = spectrum[at * stride + length:(at + 1) * stride]
                entry = (part * share + row) * order
                weight = interaction[:, entry:entry + order].astype(WIDE)
                weighted[row * stride:row * stride + length, :] = (
                    (s_re * s_re - s_im * s_im) * weight
                ).astype(LOW)
                weighted[row * stride + length:(row + 1) * stride, :] = (
                    2.0 * s_re * s_im * weight
                ).astype(LOW)
        result = dot(inverse[...], weighted[...]) * length ** -0.5
        leaving[part] = result.reshape(groups, 2, share, order).astype(LOW)
        for peer in peers:
            back(part, peer, me).start()
        own = pltpu.make_async_copy(leaving.at[part, me], landed.at[me, part], own_sem.at[1, part])
        own.start()
        returns.append(own)

    for part in range(parts):
        for peer in peers:
            go(part, peer, me).wait_send()

    @pl.when(feeds)
    def _():
        for piece in range(pieces):
            hop(piece).wait_send()

    if split:
        @pl.when(lends)
        def _():
            for piece in range(pieces):
                lend(piece).wait_send()

        @pl.when(grows)
        def _():
            for part in range(parts):
                for peer in peers + [me]:
                    late(part, peer, me // 2).wait_send()

    for part in range(parts):
        returns[part].wait()
        for peer in peers:
            back(part, peer, me).wait_send()
        for peer in peers:
            back(part, peer, peer).wait_recv()


def write(parts, landed, out_hbm, sem):
    copies = []
    for part in range(parts):
        for side in range(2):
            copy = pltpu.make_async_copy(
                landed.at[:, part, side], out_hbm.at[side, :, part], sem.at[part, side]
            )
            copy.start()
            copies.append(copy)
    for copy in copies:
        copy.wait()


def local(lesser_in, retarded, coupling, interaction):
    order = coupling.shape[-1]
    groups = lax.axis_size("energy")
    sections = lax.axis_size("space")
    length = interaction.shape[1]
    rows = order // groups
    pieces = 2
    parts = 2 if rows % 16 == 0 else 1
    share = rows // parts
    assert lesser_in.shape[0] == 1 and coupling.shape[0] == 1
    late = list(range(1, groups, 2)) if sections > 1 and groups % 2 == 0 else []
    forward = jnp.asarray(forward_matrix(list(range(groups)) + late, length, share))
    inverse = jnp.asarray(inverse_matrix(groups, length, share))
    dma = pltpu.SemaphoreType.DMA
    matrix = (2, order, order)
    spread = (parts, groups, 2 * share, order)
    landed = pl.pallas_call(
        functools.partial(kernel, sections, groups, rows, length, pieces, parts),
        out_shape=jax.ShapeDtypeStruct((groups, parts, 2, share, order), LOW),
        in_specs=[ANY] * 6,
        out_specs=pl.BlockSpec(memory_space=pltpu.VMEM),
        scratch_shapes=[
            pltpu.VMEM(matrix, LOW),
            pltpu.VMEM(matrix, LOW),
            pltpu.VMEM(matrix, LOW),
            pltpu.VMEM(interaction.shape[1:], LOW),
            pltpu.VMEM(forward.shape, LOW),
            pltpu.VMEM(inverse.shape, LOW),
            pltpu.VMEM(matrix, WIDE),
            pltpu.VMEM(matrix, LOW),
            pltpu.VMEM(matrix, LOW),
            pltpu.VMEM(matrix, LOW),
            pltpu.VMEM(matrix, LOW),
            pltpu.VMEM(matrix, LOW),
            pltpu.VMEM(spread, LOW),
            pltpu.VMEM((parts, groups + len(late), 2 * share, order), LOW),
            pltpu.VMEM(spread, LOW),
            pltpu.VMEM((share * 2 * length, order), LOW),
            pltpu.VMEM((parts, groups, 2, share, order), LOW),
            dma((6,)),
            dma((pieces,)),
            dma((pieces,)),
            dma((pieces,)),
            dma((pieces,)),
            dma((parts, groups)),
            dma((parts, groups)),
            dma((parts, groups)),
            dma((parts, max(1, len(late)))),
            dma((parts, groups)),
            dma((parts, groups)),
            dma((2, parts)),
        ],
        compiler_params=pltpu.CompilerParams(collective_id=0, has_side_effects=True),
    )(lesser_in, retarded, coupling, interaction, forward, inverse)
    out = pl.pallas_call(
        functools.partial(write, parts),
        out_shape=jax.ShapeDtypeStruct((2, groups, parts, share, order), LOW),
        in_specs=[pl.BlockSpec(memory_space=pltpu.VMEM)],
        out_specs=ANY,
        scratch_shapes=[dma((parts, 2))],
    )(landed)
    return out.reshape(1, 1, 2, order, order)


def solution(mesh):
    in_specs = (
        P("energy", "space", None, None, None),
        P("energy", "space", None, None, None),
        P("space", None, None, None),
        P("space", None, "energy"),
    )
    out_specs = P("energy", "space", None, None, None)
    return jax.shard_map(local, mesh=mesh, in_specs=in_specs, out_specs=out_specs, check_vma=False)
```

time: 28.3 us -> 28.4 us (level)
  Pallas kernels: 26.5 us -> 28.2 us
  local copies, waits for them, and re-layouts: 1.67 us -> 0 us
    pallas_call x0 -> x1, Pallas kernels: none -> 1.68 us  [local(): pl.pallas_call(functools.partial(write, parts), out_shape=jax.ShapeDtypeS...]
    transpose x1 -> x0, local copies, waits for them, and re-layouts: 1.67 us -> none  [local(): returned.reshape(groups, parts, 2, share, order).transpose(2, 0, 1, 3, 4)]
where the time goes in v1:
time: 28.4 us; the launch traced here: 28.2 us
  Pallas kernels  28.2 us (99%)
    pallas_call x1, Pallas kernels, local(): pl.pallas_call(functools.partial(kernel, sections, groups, rows, length,...  26.5 us
    pallas_call x1, Pallas kernels, local(): pl.pallas_call(functools.partial(write, parts), out_shape=jax.ShapeDtypeS...  1.68 us

profile of v1, /device:TPU:3, one launch (start us, length us, event | category | flops | bytes accessed | tf_op | source)
XLA Modules:
  0.0 28.2 jit_solution(2406863935315109270)
XLA Ops:
  0.0 26.5 %shard_map.64.landed = bf16[16,2,2,8,256]{4,3,2,1,0:T(8,128)(2,1)} custom-call(bf16[1,1,2,256,256]{4,3,2,1,0:T(8,128)(2,1)} %lesser_hbm.1, bf16[1,1,2,256,256]{4,3,2,1,0:T(8,128)(2,1)} %retarded_hbm.1, bf16[1,2,256,256]{3,2,1,0:T(8,128)(2,1)} %coupling_hbm.1, bf16[1,32,4096]{2,1,0:T(8,128)(2,1)} %interaction_hbm.1, ...), custom_call_target="tpu_custom_call" | custom-call | tf_op jit(solution)/shard_map/pallas_call | solution.py:370
  26.5 1.7 %shard_map.65 = bf16[2,16,2,8,256]{4,3,2,1,0:T(8,128)(2,1)} custom-call(bf16[16,2,2,8,256]{4,3,2,1,0:T(8,128)(2,1)} %shard_map.64.landed), custom_call_target="tpu_custom_call" | custom-call | tf_op jit(solution)/shard_map/pallas_call | solution.py:408

commit v2 on v1

--- a/solution.py
+++ b/solution.py
@@ -67,7 +67,7 @@
     lesser, retarded, coupling, interaction, forward, inverse,
     total, maps, green, before, theirs, carried, homing, homed, grown, weighted, leaving,
     load_sem, hop_send, hop_recv, map_send, map_recv, go_send, go_recv, late_send, late_recv,
-    back_send, back_recv, own_sem,
+    back_send, back_recv, turn,
 ):
     section = lax.axis_index("space")
     me = lax.axis_index("energy")
@@ -213,8 +213,8 @@
         return pltpu.make_async_remote_copy(
             src_ref=homing.at[part, peer],
             dst_ref=homed.at[part, slot],
-            send_sem=go_send.at[part, peer],
-            recv_sem=go_recv.at[part, slot],
+            send_sem=go_send,
+            recv_sem=go_recv.at[part],
             device_id={"energy": peer},
             device_id_type=MESH,
         )
@@ -223,8 +223,8 @@
         return pltpu.make_async_remote_copy(
             src_ref=grown.at[part, peer],
             dst_ref=homed.at[part, groups + slot],
-            send_sem=late_send.at[part, peer],
-            recv_sem=late_recv.at[part, slot],
+            send_sem=late_send,
+            recv_sem=late_recv.at[part],
             device_id={"space": last, "energy": peer},
             device_id_type=MESH,
         )
@@ -233,20 +233,20 @@
         return pltpu.make_async_remote_copy(
             src_ref=leaving.at[part, peer],
             dst_ref=landed.at[slot, part],
-            send_sem=back_send.at[part, peer],
-            recv_sem=back_recv.at[part, slot],
+            send_sem=back_send,
+            recv_sem=back_recv,
             device_id={"energy": peer},
             device_id_type=MESH,
         )
 
+    def drain(ref, sem):
+        pltpu.make_async_copy(ref, ref, sem).wait()
+
     scattered((total[0], total[1]), homing)
-    kept = []
     for part in range(parts):
         for peer in peers:
             go(part, peer, me).start()
-        own = pltpu.make_async_copy(homing.at[part, me], homed.at[part, me], own_sem.at[0, part])
-        own.start()
-        kept.append(own)
+        homed[part, me] = homing[part, me]
 
     if split:
         @pl.when(grows)
@@ -272,16 +272,12 @@
 
     stride = 2 * length
     chunk = max(1, order // stride)
-    returns = []
     for part in range(parts):
-        kept[part].wait()
-        for peer in peers:
-            go(part, peer, peer).wait_recv()
+        drain(homed.at[part, :groups - 1], go_recv.at[part])
         if split:
             @pl.when(is_last)
             def _():
-                for at in range(half):
-                    late(part, me, at).wait_recv()
+                drain(homed.at[part, groups:], late_recv.at[part])
         entries = homed[part]
         if 2 * share % 16:
             entries = entries.astype(WIDE)
@@ -303,15 +299,20 @@
                 ).astype(LOW)
         result = dot(inverse[...], weighted[...]) * length ** -0.5
         leaving[part] = result.reshape(groups, 2, share, order).astype(LOW)
+        if split and part == 0:
+            @pl.when(grows)
+            def _():
+                drain(grown, late_send)
+                pl.semaphore_signal(turn, inc=1, device_id={"energy": me - 1}, device_id_type=MESH)
+
+            @pl.when((section == last - 1) & ~odd)
+            def _():
+                pl.semaphore_wait(turn, 1)
         for peer in peers:
             back(part, peer, me).start()
-        own = pltpu.make_async_copy(leaving.at[part, me], landed.at[me, part], own_sem.at[1, part])
-        own.start()
-        returns.append(own)
-
-    for part in range(parts):
-        for peer in peers:
-            go(part, peer, me).wait_send()
+        landed[me, part] = leaving[part, me]
+
+    drain(homing.at[:, :groups - 1], go_send)
 
     @pl.when(feeds)
     def _():
@@ -324,31 +325,8 @@
             for piece in range(pieces):
                 lend(piece).wait_send()
 
-        @pl.when(grows)
-        def _():
-            for part in range(parts):
-                for peer in peers + [me]:
-                    late(part, peer, me // 2).wait_send()
-
-    for part in range(parts):
-        returns[part].wait()
-        for peer in peers:
-            back(part, peer, me).wait_send()
-        for peer in peers:
-            back(part, peer, peer).wait_recv()
-
-
-def write(parts, landed, out_hbm, sem):
-    copies = []
-    for part in range(parts):
-        for side in range(2):
-            copy = pltpu.make_async_copy(
-                landed.at[:, part, side], out_hbm.at[side, :, part], sem.at[part, side]
-            )
-            copy.start()
-            copies.append(copy)
-    for copy in copies:
-        copy.wait()
+    drain(leaving.at[:, :groups - 1], back_send)
+    drain(landed.at[:groups - 1], back_recv)
 
 
 def local(lesser_in, retarded, coupling, interaction):
@@ -369,7 +347,7 @@
     spread = (parts, groups, 2 * share, order)
     landed = pl.pallas_call(
         functools.partial(kernel, sections, groups, rows, length, pieces, parts),
-        out_shape=jax.ShapeDtypeStruct((groups, parts, 2, share, order), LOW),
+        out_shape=pltpu.VMEM((groups, parts, 2, share, order), LOW),
         in_specs=[ANY] * 6,
         out_specs=pl.BlockSpec(memory_space=pltpu.VMEM),
         scratch_shapes=[
@@ -395,23 +373,17 @@
             dma((pieces,)),
             dma((pieces,)),
             dma((pieces,)),
-            dma((parts, groups)),
-            dma((parts, groups)),
-            dma((parts, groups)),
-            dma((parts, max(1, len(late)))),
-            dma((parts, groups)),
-            dma((parts, groups)),
-            dma((2, parts)),
+            dma,
+            dma((parts,)),
+            dma,
+            dma((parts,)),
+            dma,
+            dma,
+            pltpu.SemaphoreType.REGULAR,
         ],
         compiler_params=pltpu.CompilerParams(collective_id=0, has_side_effects=True),
     )(lesser_in, retarded, coupling, interaction, forward, inverse)
-    out = pl.pallas_call(
-        functools.partial(write, parts),
-        out_shape=jax.ShapeDtypeStruct((2, groups, parts, share, order), LOW),
-        in_specs=[pl.BlockSpec(memory_space=pltpu.VMEM)],
-        out_specs=ANY,
-        scratch_shapes=[dma((parts, 2))],
-    )(landed)
+    out = landed.transpose(2, 0, 1, 3, 4)
     return out.reshape(1, 1, 2, order, order)
 
 

time: 28.4 us -> 23.9 us (0.84)
  Pallas kernels: 28.2 us -> 23 us
  local copies, waits for them, and re-layouts: 0 us -> 0.72 us
    pallas_call x1, Pallas kernels: 26.5 us -> 23 us  [local(): pl.pallas_call(functools.partial(kernel, sections, groups, rows, length,...]
    pallas_call x1 -> x0, Pallas kernels: 1.68 us -> none  [local(): pl.pallas_call(functools.partial(write, parts), out_shape=jax.ShapeDtypeS...]
    transpose x0 -> x1, local copies, waits for them, and re-layouts: none -> 0.72 us  [local(): out = landed.transpose(2, 0, 1, 3, 4)]
where the time goes in v2:
time: 23.9 us; the launch traced here: 23.7 us
  Pallas kernels  23 us (96%)
  local copies, waits for them, and re-layouts  0.72 us (3%)
    pallas_call x1, Pallas kernels, local(): pl.pallas_call(functools.partial(kernel, sections, groups, rows, length,...  23 us
    transpose x1, local copies, waits for them, and re-layouts, local(): out = landed.transpose(2, 0, 1, 3, 4)  0.72 us

profile of v2, /device:TPU:3, one launch (start us, length us, event | category | flops | bytes accessed | tf_op | source)
XLA Modules:
  0.0 23.7 jit_solution(427011862265972190)
XLA Ops:
  0.0 23.0 %shard_map.64 = bf16[16,2,2,8,256]{4,3,2,1,0:T(8,128)(2,1)S(1)} custom-call(bf16[1,1,2,256,256]{4,3,2,1,0:T(8,128)(2,1)} %lesser_hbm.1, bf16[1,1,2,256,256]{4,3,2,1,0:T(8,128)(2,1)} %retarded_hbm.1, bf16[1,2,256,256]{3,2,1,0:T(8,128)(2,1)} %coupling_hbm.1, bf16[1,32,4096]{2,1,0:T(8,128)(2,1)} %interaction_hbm.1, bf16[512,384]{1,0:T(8,128)(2,1)} %constant.4.clone.forward_hbm, ...), custom_call_target="tpu_custom_call" | custom-call | tf_op jit(solution)/shard_map/pallas_call | solution.py:348
  23.0 0.7 %copy.7 = bf16[2,16,2,8,256]{4,3,2,1,0:T(8,128)(2,1)} copy(bf16[2,16,2,8,256]{4,3,0,2,1:T(8,128)(2,1)S(1)} %bitcast.2) | data formatting | bytes 524288 | tf_op jit(solution)/shard_map/transpose | solution.py:386

commit v3 on v2

--- a/solution.py
+++ b/solution.py
@@ -67,7 +67,7 @@
     lesser, retarded, coupling, interaction, forward, inverse,
     total, maps, green, before, theirs, carried, homing, homed, grown, weighted, leaving,
     load_sem, hop_send, hop_recv, map_send, map_recv, go_send, go_recv, late_send, late_recv,
-    back_send, back_recv, turn,
+    back_send, back_recv, turn, ready, clear,
 ):
     section = lax.axis_index("space")
     me = lax.axis_index("energy")
@@ -88,26 +88,28 @@
     else:
         peers = [lax.rem(me + step, groups) for step in range(1, groups)]
 
+    collects = (me + section // max(last, 1)) % 2 == 1 if split else me >= 0
     barrier = pltpu.get_barrier_semaphore()
-    for peer in peers:
-        pl.semaphore_signal(barrier, inc=1, device_id={"energy": peer}, device_id_type=MESH)
+    if split:
+        for at in range(half):
+            peer = 2 * at + 1 - section // last
+
+            @pl.when(peer != me)
+            def _():
+                pl.semaphore_signal(
+                    barrier, inc=1, device_id={"energy": peer}, device_id_type=MESH
+                )
+
+        @pl.when(grows)
+        def _():
+            pl.semaphore_signal(barrier, inc=1, device_id={"space": last}, device_id_type=MESH)
+    else:
+        for peer in peers:
+            pl.semaphore_signal(barrier, inc=1, device_id={"energy": peer}, device_id_type=MESH)
 
     @pl.when(fed)
     def _():
         pl.semaphore_signal(barrier, inc=1, device_id={"space": section - 1}, device_id_type=MESH)
-
-    if split:
-        @pl.when(grows)
-        def _():
-            pl.semaphore_signal(barrier, inc=1, device_id={"space": last}, device_id_type=MESH)
-
-        @pl.when(is_last)
-        def _():
-            for at in range(half):
-                pl.semaphore_signal(
-                    barrier, inc=1,
-                    device_id={"space": last - 1, "energy": 2 * at + 1}, device_id_type=MESH,
-                )
 
     loads = []
     for at, (source, target) in enumerate((
@@ -125,12 +127,29 @@
         else:
             load.start()
 
-    def arrived():
-        pl.semaphore_wait(
-            barrier,
-            groups - 1 + jnp.where(feeds, 1, 0) + jnp.where(lends, 1, 0)
-            + jnp.where(grows, groups, 0),
-        )
+    def across():
+        @pl.when(~collects)
+        def _():
+            pl.semaphore_wait(barrier, 1)
+
+    def gathered():
+        @pl.when(collects)
+        def _():
+            pl.semaphore_wait(barrier, groups - 1 + jnp.where(feeds, 1, 0))
+            if split:
+                pl.semaphore_signal(
+                    ready, inc=1,
+                    device_id={"energy": me + 1 - 2 * (me % 2)}, device_id_type=MESH,
+                )
+
+    def told():
+        @pl.when(~collects)
+        def _():
+            pl.semaphore_wait(ready, 1)
+
+        @pl.when(lends)
+        def _():
+            pl.semaphore_signal(clear, inc=1, device_id={"space": last - 1}, device_id_type=MESH)
 
     def hop(piece):
         columns = pl.ds(piece * width, width)
@@ -164,7 +183,7 @@
     @pl.when(lends)
     def _():
         make_maps()
-        arrived()
+        across()
         for piece in range(pieces):
             lend(piece).start()
 
@@ -176,7 +195,8 @@
 
     @pl.when(~lends)
     def _():
-        arrived()
+        across()
+        gathered()
 
     @pl.when(fed)
     def _():
@@ -243,6 +263,8 @@
         pltpu.make_async_copy(ref, ref, sem).wait()
 
     scattered((total[0], total[1]), homing)
+    if split:
+        told()
     for part in range(parts):
         for peer in peers:
             go(part, peer, me).start()
@@ -258,6 +280,7 @@
                 carried[0, part, :], carried[1, part, :] = k_re.astype(LOW), k_im.astype(LOW)
             g_re, g_im = product_adjoint(carried[0], carried[1], theirs[0], theirs[1])
             scattered((g_re, g_im), grown)
+            pl.semaphore_wait(clear, 1)
             for part in range(parts):
                 for peer in peers + [me]:
                     late(part, peer, me // 2).start()
@@ -380,6 +403,8 @@
             dma,
             dma,
             pltpu.SemaphoreType.REGULAR,
+            pltpu.SemaphoreType.REGULAR,
+            pltpu.SemaphoreType.REGULAR,
         ],
         compiler_params=pltpu.CompilerParams(collective_id=0, has_side_effects=True),
     )(lesser_in, retarded, coupling, interaction, forward, inverse)

time: 23.9 us -> 23 us (0.962)
  Pallas kernels: 23 us -> 22 us
    pallas_call x1, Pallas kernels: 23 us -> 22 us  [local(): pl.pallas_call(functools.partial(kernel, sections, groups, rows, length,...]
where the time goes in v3:
time: 23 us; the launch traced here: 22.7 us
  Pallas kernels  22 us (96%)
  local copies, waits for them, and re-layouts  0.72 us (3%)
    pallas_call x1, Pallas kernels, local(): pl.pallas_call(functools.partial(kernel, sections, groups, rows, length,...  22 us
    transpose x1, local copies, waits for them, and re-layouts, local(): out = landed.transpose(2, 0, 1, 3, 4)  0.72 us

profile of v3, /device:TPU:3, one launch (start us, length us, event | category | flops | bytes accessed | tf_op | source)
XLA Modules:
  0.0 22.7 jit_solution(10439895901681394544)
XLA Ops:
  0.0 22.0 %shard_map.64 = bf16[16,2,2,8,256]{4,3,2,1,0:T(8,128)(2,1)S(1)} custom-call(bf16[1,1,2,256,256]{4,3,2,1,0:T(8,128)(2,1)} %lesser_hbm.1, bf16[1,1,2,256,256]{4,3,2,1,0:T(8,128)(2,1)} %retarded_hbm.1, bf16[1,2,256,256]{3,2,1,0:T(8,128)(2,1)} %coupling_hbm.1, bf16[1,32,4096]{2,1,0:T(8,128)(2,1)} %interaction_hbm.1, bf16[512,384]{1,0:T(8,128)(2,1)} %constant.4.clone.forward_hbm, ...), custom_call_target="tpu_custom_call" | custom-call | tf_op jit(solution)/shard_map/pallas_call | solution.py:371
  22.0 0.7 %copy.7 = bf16[2,16,2,8,256]{4,3,2,1,0:T(8,128)(2,1)} copy(bf16[2,16,2,8,256]{4,3,0,2,1:T(8,128)(2,1)S(1)} %bitcast.2) | data formatting | bytes 524288 | tf_op jit(solution)/shard_map/transpose | solution.py:411

commit v4 on v3

--- a/solution.py
+++ b/solution.py
@@ -51,6 +51,10 @@
     return dot_t(a_re, b_re) + dot_t(a_im, b_im), dot_t(a_im, b_re) + dot_t(-a_re, b_im)
 
 
+def beside(first, second, axis):
+    return jnp.concatenate([first, second], axis=axis)
+
+
 def flipped(index, mask):
     bit = 1
     while bit <= mask:
@@ -65,9 +69,9 @@
     lesser_hbm, retarded_hbm, coupling_hbm, interaction_hbm, forward_hbm, inverse_hbm,
     landed,
     lesser, retarded, coupling, interaction, forward, inverse,
-    total, maps, green, before, theirs, carried, homing, homed, grown, weighted, leaving,
+    total, maps, green, before, theirs, carried, homing, homed, grown, repaid, weighted, leaving, passing,
     load_sem, hop_send, hop_recv, map_send, map_recv, go_send, go_recv, late_send, late_recv,
-    back_send, back_recv, turn, ready, clear,
+    pay_send, pay_recv, back_send, back_recv, relay_send, relay_recv, pass_send, turn, ready, clear,
 ):
     section = lax.axis_index("space")
     me = lax.axis_index("energy")
@@ -76,6 +80,9 @@
     last = sections - 1
     split = sections > 1 and groups % 2 == 0
     half = groups // 2 if split else 0
+    direct = parts - parts // 4
+    relays = split and groups % 4 == 0 and groups & (groups - 1) == 0
+    quarter = groups // 4 if relays else 0
     odd = me % 2 == 1 if split else me < 0
     is_last = section == last
     feeds = (section < last - 1) | ((section == last - 1) & ~odd)
@@ -87,29 +94,16 @@
         peers = [flipped(me, mask) for mask in range(groups - 1, 0, -1)]
     else:
         peers = [lax.rem(me + step, groups) for step in range(1, groups)]
-
-    collects = (me + section // max(last, 1)) % 2 == 1 if split else me >= 0
-    barrier = pltpu.get_barrier_semaphore()
-    if split:
-        for at in range(half):
-            peer = 2 * at + 1 - section // last
-
-            @pl.when(peer != me)
-            def _():
-                pl.semaphore_signal(
-                    barrier, inc=1, device_id={"energy": peer}, device_id_type=MESH
-                )
-
-        @pl.when(grows)
-        def _():
-            pl.semaphore_signal(barrier, inc=1, device_id={"space": last}, device_id_type=MESH)
-    else:
-        for peer in peers:
-            pl.semaphore_signal(barrier, inc=1, device_id={"energy": peer}, device_id_type=MESH)
-
-    @pl.when(fed)
-    def _():
-        pl.semaphore_signal(barrier, inc=1, device_id={"space": section - 1}, device_id_type=MESH)
+    homeward, mirrored = peers, 0
+    if relays:
+        own, low = me // quarter, me % quarter
+        over = 2 * (1 - own // 2)
+        mirrored = (over + 1) * quarter
+        homeward = [
+            to * quarter + flipped(low, mask)
+            for to in (over + 1, over, own + 1 - 2 * (own % 2), own)
+            for mask in range(quarter - 1, -1, -1)
+        ][:-1]
 
     loads = []
     for at, (source, target) in enumerate((
@@ -124,8 +118,31 @@
         loads.append(load)
         if target is coupling:
             pl.when(section > 0)(load.start)
-        else:
+        elif at < 2:
             load.start()
+
+    collects = (me + section // max(last, 1)) % 2 == 1 if split else me >= 0
+    barrier = pltpu.get_barrier_semaphore()
+    if split:
+        for at in range(half):
+            peer = 2 * at + 1 - section // last
+
+            @pl.when(peer != me)
+            def _():
+                pl.semaphore_signal(
+                    barrier, inc=1, device_id={"energy": peer}, device_id_type=MESH
+                )
+
+        @pl.when(grows)
+        def _():
+            pl.semaphore_signal(barrier, inc=1, device_id={"space": last}, device_id_type=MESH)
+    else:
+        for peer in peers:
+            pl.semaphore_signal(barrier, inc=1, device_id={"energy": peer}, device_id_type=MESH)
+
+    @pl.when(fed)
+    def _():
+        pl.semaphore_signal(barrier, inc=1, device_id={"space": section - 1}, device_id_type=MESH)
 
     def across():
         @pl.when(~collects)
@@ -188,6 +205,8 @@
             lend(piece).start()
 
     loads[1].wait()
+    for load in loads[3:]:
+        load.start()
     r_re, r_im = retarded[0], retarded[1]
     half_re, half_im = product(r_re, r_im, lesser[0], lesser[1])
     half_re, half_im = half_re.astype(LOW), half_im.astype(LOW)
@@ -222,12 +241,15 @@
 
     share = rows // parts
 
+    def entries_of(values, part):
+        sides = [
+            values[side].reshape(groups, parts, share, order)[:, part] for side in range(2)
+        ]
+        return beside(*sides, 1)
+
     def scattered(values, target):
         for part in range(parts):
-            target[part] = jnp.concatenate(
-                [values[side].reshape(groups, parts, share, order)[:, part] for side in range(2)],
-                axis=1,
-            ).astype(LOW).reshape(groups, 2 * share, order)
+            target[part] = entries_of(values, part).astype(LOW)
 
     def go(part, peer, slot):
         return pltpu.make_async_remote_copy(
@@ -249,10 +271,20 @@
             device_id_type=MESH,
         )
 
+    def pay():
+        return pltpu.make_async_remote_copy(
+            src_ref=grown.at[direct:],
+            dst_ref=repaid,
+            send_sem=pay_send,
+            recv_sem=pay_recv,
+            device_id={"space": last},
+            device_id_type=MESH,
+        )
+
     def back(part, peer, slot):
         return pltpu.make_async_remote_copy(
-            src_ref=leaving.at[part, peer],
-            dst_ref=landed.at[slot, part],
+            src_ref=leaving.at[part * groups + peer],
+            dst_ref=landed.at[:, slot, part],
             send_sem=back_send,
             recv_sem=back_recv,
             device_id={"energy": peer},
@@ -262,13 +294,40 @@
     def drain(ref, sem):
         pltpu.make_async_copy(ref, ref, sem).wait()
 
+    def relay():
+        return pltpu.make_async_remote_copy(
+            src_ref=leaving.at[pl.ds(mirrored, max(1, quarter))],
+            dst_ref=passing,
+            send_sem=relay_send,
+            recv_sem=relay_recv,
+            device_id={"space": last - 1},
+            device_id_type=MESH,
+        )
+
+    def forward_on(at):
+        return pltpu.make_async_remote_copy(
+            src_ref=passing.at[at],
+            dst_ref=landed.at[:, me, 0],
+            send_sem=pass_send,
+            recv_sem=back_recv,
+            device_id={"space": last, "energy": mirrored + at},
+            device_id_type=MESH,
+        )
+
     scattered((total[0], total[1]), homing)
     if split:
         told()
-    for part in range(parts):
-        for peer in peers:
+
+    def send(part):
+        for peer in homeward:
             go(part, peer, me).start()
         homed[part, me] = homing[part, me]
+
+    for part in range(parts):
+        if split and part >= direct:
+            pl.when(~lends)(functools.partial(send, part))
+        else:
+            send(part)
 
     if split:
         @pl.when(grows)
@@ -281,14 +340,27 @@
             g_re, g_im = product_adjoint(carried[0], carried[1], theirs[0], theirs[1])
             scattered((g_re, g_im), grown)
             pl.semaphore_wait(clear, 1)
-            for part in range(parts):
+            if direct < parts:
+                pay().start()
+            for part in range(direct):
                 for peer in peers + [me]:
                     late(part, peer, me // 2).start()
 
         @pl.when(~is_last)
         def _():
-            for part in range(parts):
+            for part in range(direct):
                 homed[part, groups:] = jnp.zeros((half, 2 * share, order), LOW)
+
+        if direct < parts:
+            @pl.when(lends)
+            def _():
+                pay().wait_recv()
+                for part in range(direct, parts):
+                    homing[part] = (
+                        entries_of((total[0], total[1]), part)
+                        + repaid[part - direct].astype(WIDE)
+                    ).astype(LOW)
+                    send(part)
 
     for load in loads[3:]:
         load.wait()
@@ -297,16 +369,19 @@
     chunk = max(1, order // stride)
     for part in range(parts):
         drain(homed.at[part, :groups - 1], go_recv.at[part])
-        if split:
+        if split and part < direct:
             @pl.when(is_last)
             def _():
                 drain(homed.at[part, groups:], late_recv.at[part])
-        entries = homed[part]
+        count = groups + half if part < direct else groups
+        entries = homed[part, :count]
         if 2 * share % 16:
             entries = entries.astype(WIDE)
-        entries = entries.reshape((groups + half) * 2 * share, order).astype(LOW)
+        entries = entries.reshape(count * 2 * share, order).astype(LOW)
         for first in range(0, share, chunk):
-            spectrum = dot(forward[first * stride:(first + chunk) * stride, :], entries)
+            spectrum = dot(
+                forward[first * stride:(first + chunk) * stride, :count * 2 * share], entries
+            )
             spectrum = spectrum * groups ** -0.5
             for at in range(chunk):
                 row = first + at
@@ -321,19 +396,42 @@
                     2.0 * s_re * s_im * weight
                 ).astype(LOW)
         result = dot(inverse[...], weighted[...]) * length ** -0.5
-        leaving[part] = result.reshape(groups, 2, share, order).astype(LOW)
+        leaving[part * groups:(part + 1) * groups] = (
+            result.reshape(groups, 2, share, order).astype(LOW)
+        )
         if split and part == 0:
             @pl.when(grows)
             def _():
-                drain(grown, late_send)
+                drain(grown.at[:direct], late_send)
                 pl.semaphore_signal(turn, inc=1, device_id={"energy": me - 1}, device_id_type=MESH)
 
             @pl.when((section == last - 1) & ~odd)
             def _():
                 pl.semaphore_wait(turn, 1)
-        for peer in peers:
+        here = homeward
+        if relays:
+            here = homeward[quarter:2 * quarter] + homeward[2 * quarter:]
+            if part == 0:
+                @pl.when(is_last)
+                def _():
+                    relay().start()
+
+                @pl.when(~is_last)
+                def _():
+                    for peer in homeward[:quarter]:
+                        back(part, peer, me).start()
+            else:
+                here = here[:quarter] + homeward[:quarter] + here[quarter:]
+        for peer in here:
             back(part, peer, me).start()
-        landed[me, part] = leaving[part, me]
+        landed[:, me, part] = leaving[part * groups + me]
+
+    if relays:
+        @pl.when(section == last - 1)
+        def _():
+            relay().wait_recv()
+            for at in range(quarter):
+                forward_on(at).start()
 
     drain(homing.at[:, :groups - 1], go_send)
 
@@ -348,8 +446,27 @@
             for piece in range(pieces):
                 lend(piece).wait_send()
 
-    drain(leaving.at[:, :groups - 1], back_send)
-    drain(landed.at[:groups - 1], back_recv)
+        if direct < parts:
+            @pl.when(grows)
+            def _():
+                pay().wait_send()
+
+    if relays:
+        @pl.when(section == last - 1)
+        def _():
+            drain(passing, pass_send)
+
+        @pl.when(is_last)
+        def _():
+            relay().wait_send()
+            drain(leaving.at[:parts * (groups - 1) - quarter], back_send)
+
+        @pl.when(~is_last)
+        def _():
+            drain(leaving.at[:parts * (groups - 1)], back_send)
+    else:
+        drain(leaving.at[:parts * (groups - 1)], back_send)
+    drain(landed.at[:, :groups - 1], back_recv)
 
 
 def local(lesser_in, retarded, coupling, interaction):
@@ -359,7 +476,7 @@
     length = interaction.shape[1]
     rows = order // groups
     pieces = 2
-    parts = 2 if rows % 16 == 0 else 1
+    parts = 4 if rows % 16 == 0 else 1
     share = rows // parts
     assert lesser_in.shape[0] == 1 and coupling.shape[0] == 1
     late = list(range(1, groups, 2)) if sections > 1 and groups % 2 == 0 else []
@@ -370,7 +487,7 @@
     spread = (parts, groups, 2 * share, order)
     landed = pl.pallas_call(
         functools.partial(kernel, sections, groups, rows, length, pieces, parts),
-        out_shape=pltpu.VMEM((groups, parts, 2, share, order), LOW),
+        out_shape=pltpu.VMEM((2, groups, parts, share, order), LOW),
         in_specs=[ANY] * 6,
         out_specs=pl.BlockSpec(memory_space=pltpu.VMEM),
         scratch_shapes=[
@@ -389,8 +506,10 @@
             pltpu.VMEM(spread, LOW),
             pltpu.VMEM((parts, groups + len(late), 2 * share, order), LOW),
             pltpu.VMEM(spread, LOW),
+            pltpu.VMEM((max(1, parts // 4), groups, 2 * share, order), LOW),
             pltpu.VMEM((share * 2 * length, order), LOW),
-            pltpu.VMEM((parts, groups, 2, share, order), LOW),
+            pltpu.VMEM((parts * groups, 2, share, order), LOW),
+            pltpu.VMEM((max(1, groups // 4), 2, share, order), LOW),
             dma((6,)),
             dma((pieces,)),
             dma((pieces,)),
@@ -400,6 +519,11 @@
             dma((parts,)),
             dma,
             dma((parts,)),
+            dma,
+            dma,
+            dma,
+            dma,
+            dma,
             dma,
             dma,
             pltpu.SemaphoreType.REGULAR,
@@ -408,8 +532,7 @@
         ],
         compiler_params=pltpu.CompilerParams(collective_id=0, has_side_effects=True),
     )(lesser_in, retarded, coupling, interaction, forward, inverse)
-    out = landed.transpose(2, 0, 1, 3, 4)
-    return out.reshape(1, 1, 2, order, order)
+    return landed.reshape(1, 1, 2, order, order)
 
 
 def solution(mesh):

time: 23 us -> 22.4 us (0.974)
  Pallas kernels: 22 us -> 21.5 us
    reshape x0 -> x1, local copies, waits for them, and re-layouts: none -> 0.77 us  [local(): return landed.reshape(1, 1, 2, order, order)]
    transpose x1 -> x0, local copies, waits for them, and re-layouts: 0.72 us -> none  [local(): out = landed.transpose(2, 0, 1, 3, 4)]
    pallas_call x1, Pallas kernels: 22 us -> 21.5 us  [local(): pl.pallas_call(functools.partial(kernel, sections, groups, rows, length,...]
where the time goes in v4:
time: 22.4 us; the launch traced here: 22.2 us
  Pallas kernels  21.5 us (96%)
  local copies, waits for them, and re-layouts  0.77 us (3%)
    pallas_call x1, Pallas kernels, local(): pl.pallas_call(functools.partial(kernel, sections, groups, rows, length,...  21.5 us
    reshape x1, local copies, waits for them, and re-layouts, local(): return landed.reshape(1, 1, 2, order, order)  0.77 us

profile of v4, /device:TPU:3, one launch (start us, length us, event | category | flops | bytes accessed | tf_op | source)
XLA Modules:
  0.0 22.2 jit_solution(838299663262207824)
XLA Ops:
  0.0 21.5 %shard_map.64 = bf16[2,16,4,4,256]{4,3,2,1,0:T(4,128)(2,1)S(1)} custom-call(bf16[1,1,2,256,256]{4,3,2,1,0:T(8,128)(2,1)} %lesser_hbm.1, bf16[1,1,2,256,256]{4,3,2,1,0:T(8,128)(2,1)} %retarded_hbm.1, bf16[1,2,256,256]{3,2,1,0:T(8,128)(2,1)} %coupling_hbm.1, bf16[1,32,4096]{2,1,0:T(8,128)(2,1)} %interaction_hbm.1, bf16[256,192]{1,0:T(8,128)(2,1)} %constant.4.clone.forward_hbm, ...), custom_call_target="tpu_custom_call" | custom-call | tf_op jit(solution)/shard_map/pallas_call | solution.py:488
  21.5 0.8 %reshape.3 = bf16[1,1,2,256,256]{4,3,2,1,0:T(8,128)(2,1)} reshape(bf16[2,16,4,4,256]{4,3,2,1,0:T(4,128)(2,1)S(1)} %shard_map.64) | data formatting | bytes 524288 | tf_op jit(solution)/shard_map/reshape | solution.py:535

commit v5 on v4

--- a/solution.py
+++ b/solution.py
@@ -405,12 +405,27 @@
                 drain(grown.at[:direct], late_send)
                 pl.semaphore_signal(turn, inc=1, device_id={"energy": me - 1}, device_id_type=MESH)
 
+            if relays:
+                @pl.when(grows & (me // quarter == 1))
+                def _():
+                    for peer in (me - quarter, me - quarter - 1):
+                        pl.semaphore_signal(
+                            turn, inc=1, device_id={"energy": peer}, device_id_type=MESH
+                        )
+
+                @pl.when(grows & (me // quarter == 0))
+                def _():
+                    pl.semaphore_wait(turn, 1)
+
             @pl.when((section == last - 1) & ~odd)
             def _():
-                pl.semaphore_wait(turn, 1)
-        here = homeward
+                first = me // quarter == 0 if relays else me < 0
+                pl.semaphore_wait(turn, jnp.where(first, 2, 1))
+        sends = [(part, peer) for peer in homeward]
         if relays:
-            here = homeward[quarter:2 * quarter] + homeward[2 * quarter:]
+            upper, lower, near = (
+                homeward[:quarter], homeward[quarter:2 * quarter], homeward[2 * quarter:]
+            )
             if part == 0:
                 @pl.when(is_last)
                 def _():
@@ -418,12 +433,17 @@
 
                 @pl.when(~is_last)
                 def _():
-                    for peer in homeward[:quarter]:
+                    for peer in upper:
                         back(part, peer, me).start()
-            else:
-                here = here[:quarter] + homeward[:quarter] + here[quarter:]
-        for peer in here:
-            back(part, peer, me).start()
+            waiting = list(range(1, parts - 1))
+            at_last = waiting + [part] if part == parts - 1 else [part]
+            if part == 0 or part in waiting:
+                at_last = []
+            crossing = [(which, peer) for which in at_last for peer in upper]
+            home = [(part, peer) for peer in near]
+            sends = [(part, peer) for peer in lower] + crossing + home
+        for which, peer in sends:
+            back(which, peer, me).start()
         landed[:, me, part] = leaving[part * groups + me]
 
     if relays:

time: 22.4 us -> 21.9 us (0.978)
  the two profiles are of different devices: /device:TPU:3 before, /device:TPU:11 now
where the time goes in v5:
time: 21.9 us; the launch traced here: 21.7 us
  Pallas kernels  20.9 us (95%)
  local copies, waits for them, and re-layouts  0.77 us (4%)
    pallas_call x1, Pallas kernels, local(): pl.pallas_call(functools.partial(kernel, sections, groups, rows, length,...  20.9 us
    reshape x1, local copies, waits for them, and re-layouts, local(): return landed.reshape(1, 1, 2, order, order)  0.77 us

profile of v5, /device:TPU:11, one launch (start us, length us, event | category | flops | bytes accessed | tf_op | source)
XLA Modules:
  0.0 21.7 jit_solution(14016002649230296001)
XLA Ops:
  0.0 20.9 %shard_map.64 = bf16[2,16,4,4,256]{4,3,2,1,0:T(4,128)(2,1)S(1)} custom-call(bf16[1,1,2,256,256]{4,3,2,1,0:T(8,128)(2,1)} %lesser_hbm.1, bf16[1,1,2,256,256]{4,3,2,1,0:T(8,128)(2,1)} %retarded_hbm.1, bf16[1,2,256,256]{3,2,1,0:T(8,128)(2,1)} %coupling_hbm.1, bf16[1,32,4096]{2,1,0:T(8,128)(2,1)} %interaction_hbm.1, bf16[256,192]{1,0:T(8,128)(2,1)} %constant.4.clone.forward_hbm, ...), custom_call_target="tpu_custom_call" | custom-call | tf_op jit(solution)/shard_map/pallas_call | solution.py:508
  21.0 0.8 %reshape.3 = bf16[1,1,2,256,256]{4,3,2,1,0:T(8,128)(2,1)} reshape(bf16[2,16,4,4,256]{4,3,2,1,0:T(4,128)(2,1)S(1)} %shard_map.64) | data formatting | bytes 524288 | tf_op jit(solution)/shard_map/reshape | solution.py:555

commit v6 on v5

--- a/solution.py
+++ b/solution.py
@@ -70,7 +70,7 @@
     landed,
     lesser, retarded, coupling, interaction, forward, inverse,
     total, maps, green, before, theirs, carried, homing, homed, grown, repaid, weighted, leaving, passing,
-    load_sem, hop_send, hop_recv, map_send, map_recv, go_send, go_recv, late_send, late_recv,
+    load_sem, hop_send, hop_recv, map_send, map_recv, go_send, go_recv, late_send,
     pay_send, pay_recv, back_send, back_recv, relay_send, relay_recv, pass_send, turn, ready, clear,
 ):
     section = lax.axis_index("space")
@@ -266,7 +266,7 @@
             src_ref=grown.at[part, peer],
             dst_ref=homed.at[part, groups + slot],
             send_sem=late_send,
-            recv_sem=late_recv.at[part],
+            recv_sem=go_recv.at[part],
             device_id={"space": last, "energy": peer},
             device_id_type=MESH,
         )
@@ -368,11 +368,15 @@
     stride = 2 * length
     chunk = max(1, order // stride)
     for part in range(parts):
-        drain(homed.at[part, :groups - 1], go_recv.at[part])
         if split and part < direct:
-            @pl.when(is_last)
-            def _():
-                drain(homed.at[part, groups:], late_recv.at[part])
+            pl.when(is_last)(
+                functools.partial(drain, homed.at[part, :groups + half - 1], go_recv.at[part])
+            )
+            pl.when(~is_last)(
+                functools.partial(drain, homed.at[part, :groups - 1], go_recv.at[part])
+            )
+        else:
+            drain(homed.at[part, :groups - 1], go_recv.at[part])
         count = groups + half if part < direct else groups
         entries = homed[part, :count]
         if 2 * share % 16:
@@ -495,7 +499,7 @@
     sections = lax.axis_size("space")
     length = interaction.shape[1]
     rows = order // groups
-    pieces = 2
+    pieces = 1
     parts = 4 if rows % 16 == 0 else 1
     share = rows // parts
     assert lesser_in.shape[0] == 1 and coupling.shape[0] == 1
@@ -538,7 +542,6 @@
             dma,
             dma((parts,)),
             dma,
-            dma((parts,)),
             dma,
             dma,
             dma,

time: 21.9 us -> 21.8 us (level)
  no operation moved by 1% of the time
where the time goes in v6:
time: 21.8 us; the launch traced here: 21.6 us
  Pallas kernels  20.9 us (96%)
  local copies, waits for them, and re-layouts  0.77 us (4%)
    pallas_call x1, Pallas kernels, local(): pl.pallas_call(functools.partial(kernel, sections, groups, rows, length,...  20.9 us
    reshape x1, local copies, waits for them, and re-layouts, local(): return landed.reshape(1, 1, 2, order, order)  0.77 us

profile of v6, /device:TPU:11, one launch (start us, length us, event | category | flops | bytes accessed | tf_op | source)
XLA Modules:
  0.0 21.6 jit_solution(18306371428943866813)
XLA Ops:
  0.0 20.9 %shard_map.64 = bf16[2,16,4,4,256]{4,3,2,1,0:T(4,128)(2,1)S(1)} custom-call(bf16[1,1,2,256,256]{4,3,2,1,0:T(8,128)(2,1)} %lesser_hbm.1, bf16[1,1,2,256,256]{4,3,2,1,0:T(8,128)(2,1)} %retarded_hbm.1, bf16[1,2,256,256]{3,2,1,0:T(8,128)(2,1)} %coupling_hbm.1, bf16[1,32,4096]{2,1,0:T(8,128)(2,1)} %interaction_hbm.1, bf16[256,192]{1,0:T(8,128)(2,1)} %constant.4.clone.forward_hbm, ...), custom_call_target="tpu_custom_call" | custom-call | tf_op jit(solution)/shard_map/pallas_call | solution.py:512
  20.9 0.8 %reshape.3 = bf16[1,1,2,256,256]{4,3,2,1,0:T(8,128)(2,1)} reshape(bf16[2,16,4,4,256]{4,3,2,1,0:T(4,128)(2,1)S(1)} %shard_map.64) | data formatting | bytes 524288 | tf_op jit(solution)/shard_map/reshape | solution.py:558

commit v7 on v5

--- a/solution.py
+++ b/solution.py
@@ -431,10 +431,6 @@
                 def _():
                     relay().start()
 
-                @pl.when(~is_last)
-                def _():
-                    for peer in upper:
-                        back(part, peer, me).start()
             waiting = list(range(1, parts - 1))
             at_last = waiting + [part] if part == parts - 1 else [part]
             if part == 0 or part in waiting:
@@ -444,6 +440,11 @@
             sends = [(part, peer) for peer in lower] + crossing + home
         for which, peer in sends:
             back(which, peer, me).start()
+        if relays and part == parts - 1:
+            @pl.when(~is_last)
+            def _():
+                for peer in homeward[:quarter]:
+                    back(0, peer, me).start()
         landed[:, me, part] = leaving[part * groups + me]
 
     if relays:

time: 21.9 us -> 21.9 us (level)
  no operation moved by 1% of the time
where the time goes in v7:
time: 21.9 us; the launch traced here: 21.7 us
  Pallas kernels  20.9 us (95%)
  local copies, waits for them, and re-layouts  0.77 us (4%)
    pallas_call x1, Pallas kernels, local(): pl.pallas_call(functools.partial(kernel, sections, groups, rows, length,...  20.9 us
    reshape x1, local copies, waits for them, and re-layouts, local(): return landed.reshape(1, 1, 2, order, order)  0.77 us

profile of v7, /device:TPU:11, one launch (start us, length us, event | category | flops | bytes accessed | tf_op | source)
XLA Modules:
  0.0 21.7 jit_solution(8513288974249402443)
XLA Ops:
  0.0 20.9 %shard_map.64 = bf16[2,16,4,4,256]{4,3,2,1,0:T(4,128)(2,1)S(1)} custom-call(bf16[1,1,2,256,256]{4,3,2,1,0:T(8,128)(2,1)} %lesser_hbm.1, bf16[1,1,2,256,256]{4,3,2,1,0:T(8,128)(2,1)} %retarded_hbm.1, bf16[1,2,256,256]{3,2,1,0:T(8,128)(2,1)} %coupling_hbm.1, bf16[1,32,4096]{2,1,0:T(8,128)(2,1)} %interaction_hbm.1, bf16[256,192]{1,0:T(8,128)(2,1)} %constant.4.clone.forward_hbm, ...), custom_call_target="tpu_custom_call" | custom-call | tf_op jit(solution)/shard_map/pallas_call | solution.py:509
  21.0 0.8 %reshape.3 = bf16[1,1,2,256,256]{4,3,2,1,0:T(8,128)(2,1)} reshape(bf16[2,16,4,4,256]{4,3,2,1,0:T(4,128)(2,1)S(1)} %shard_map.64) | data formatting | bytes 524288 | tf_op jit(solution)/shard_map/reshape | solution.py:556
